TPU v7x, 1024 devices: a whole 4x8x16 slice. The times are simulated.
1024 devices in a mesh: section: 2 (over core), group: 8 (over y), expert: 64 (over x, z).
Axes of the slice: x: 4, y: 8, z: 16, core: 2. Of those that a mesh axis runs over, the one named last changes fastest.
Arguments:
- tokens: bfloat16 [16, 4096, 2048], P('group', 'expert'), parts along dimension 0
- chosen: int32 [2, 16, 8, 64], P('section', 'group'), parts along dimension 1, may hold values from 0 to 4095, as said below
- norm_gain: float32 [2, 2048], P('section'), may hold values from 0.25 to 1.75
- router: bfloat16 [2, 2048, 8], P('section'), may hold values from -0.25 to 0.25
- w_in: bfloat16 [2, 64, 2048, 1024], P('section', 'expert'), may hold values from -0.125 to 0.125
- w_out: bfloat16 [2, 64, 1024, 2048], P('section', 'expert'), may hold values from -0.0625 to 0.0625
Outputs:
- outputs: bfloat16 [2, 16, 4096, 2048], P('section', 'group', 'expert'), parts along dimension 1
There are 8 independent parts, one for each index of `group`. A program takes and returns all parts, laid end to end along the dimension named above; an argument that names none is the same for every part. Nothing has to cross between parts.
Inputs may be any that keep to these rules, and one draw needn't show every extreme that they name: `chosen`: for each section, micro-batch and expert the 64 indices are distinct and in no particular order. Of one device's tokens (an aligned block of 64 indices) an expert chooses at most 2; in every draw some expert chooses exactly 2 from some block.
All inputs are finite; a program needn't handle non-finite values.
Results may differ from a plain program's by a relative error of at most 0.001.
Values may be sent and summed in bfloat16 or wider, within the bound.
No kernel may reach another device: no remote copies, remote signals or barrier semaphores. Data moves between devices by JAX's collectives and lax.ppermute only.
A program may use at most 64 MiB of HBM per device.

v0:
```python
import jax
import jax.numpy as jnp
from jax import lax
from jax.sharding import PartitionSpec as P


def passed_along(value, axis, steps):
    count = lax.axis_size(axis)
    leading, last = (max(0, -steps), min(count, count - steps))
    return lax.ppermute(value, axis, [(source, source + steps) for source in range(leading, last)])


def moe_layer(
    current, picks_now, gain_row, router_cols, w_first, w_second, device, owners, shards_each
):
    tok_rows, width = current.shape
    experts, capacity = picks_now.shape
    slots = 2 * capacity // owners
    floats = current.astype(jnp.float32)
    inverse_rms = lax.rsqrt(jnp.mean(floats * floats, axis=-1, keepdims=True) + 1e-06)
    normed = (floats * inverse_rms * gain_row).astype(jnp.bfloat16)
    gate_all = jax.nn.sigmoid(jnp.dot(normed, router_cols, preferred_element_type=jnp.float32))
    owner_of = picks_now // tok_rows
    onehot = (owner_of[:, :, None] == jnp.arange(owners, dtype=jnp.int32)[None, None, :]).astype(
        jnp.int32
    )
    order_slot = jnp.cumsum(onehot, axis=1) - 1
    slot_of = jnp.sum(order_slot * onehot, axis=2)
    is_mine = owner_of == device
    local_idx = picks_now - device * tok_rows
    slot_hit = (
        (slot_of[:, :, None] == jnp.arange(slots, dtype=jnp.int32)[None, None, :])
        & is_mine[:, :, None]
    ).astype(jnp.float32)
    tok_hit = (
        local_idx[:, :, None] == jnp.arange(tok_rows, dtype=jnp.int32)[None, None, :]
    ).astype(jnp.float32)
    selector = jnp.einsum("xcs,xct->xst", slot_hit, tok_hit)
    flat_select = selector.reshape(experts * slots, tok_rows)
    gate_slot = jnp.einsum("xst,tx->xs", selector, gate_all, precision=lax.Precision.HIGHEST)
    dispatched = jnp.dot(
        flat_select.astype(jnp.bfloat16), normed, preferred_element_type=jnp.float32
    ).astype(jnp.bfloat16)
    outgoing = jnp.broadcast_to(
        dispatched.reshape(experts, 1, slots, width), (experts, shards_each, slots, width)
    ).reshape(owners, slots, width)
    arrived = lax.all_to_all(outgoing, "expert", split_axis=0, concat_axis=0, tiled=True)
    item_count = arrived.shape[1]
    flat_rows = arrived.reshape(-1, width)
    hidden = jax.nn.gelu(
        jnp.dot(flat_rows, w_first, preferred_element_type=jnp.float32), approximate=True
    ).astype(jnp.bfloat16)
    partial_value = jnp.dot(hidden, w_second, preferred_element_type=jnp.float32).reshape(
        owners, item_count, width
    )
    returned = lax.all_to_all(partial_value, "expert", split_axis=0, concat_axis=0, tiled=True)
    summed = returned.reshape(experts, shards_each, slots, width).sum(axis=1)
    weighted = summed * gate_slot[:, :, None]
    contrib = jnp.dot(
        flat_select.T, weighted.reshape(experts * slots, width), precision=lax.Precision.HIGHEST
    )
    return (floats + contrib).astype(jnp.bfloat16)


def local(tokens, chosen, norm_gain, router, w_in, w_out):
    sections = lax.axis_size("section")
    owners = lax.axis_size("expert")
    section_index = lax.axis_index("section")
    device = lax.axis_index("expert")
    micro_count, tok_rows, width = tokens.shape
    experts = chosen.shape[2]
    shards_each = owners // experts
    gain_row = norm_gain[0]
    router_cols = router[0]
    w_first = w_in[0, 0]
    w_second = w_out[0, 0]
    outputs = jnp.zeros((1, micro_count, tok_rows, width), jnp.bfloat16)
    received = jnp.zeros((tok_rows, width), jnp.bfloat16)
    tick_count = micro_count + sections - 1
    for tick_index in range(tick_count):
        batch_index = tick_index - section_index
        clipped = jnp.clip(batch_index, 0, micro_count - 1)
        fresh_input = tokens[min(tick_index, micro_count - 1)]
        current = jnp.where(section_index == 0, fresh_input, received)
        picks_now = lax.dynamic_index_in_dim(chosen[0], clipped, 0, keepdims=False)
        layer_out = moe_layer(
            current,
            picks_now,
            gain_row,
            router_cols,
            w_first,
            w_second,
            device,
            owners,
            shards_each,
        )
        in_range = (batch_index >= 0) & (batch_index < micro_count)
        previous = lax.dynamic_index_in_dim(outputs[0], clipped, 0, keepdims=False)
        written = jnp.where(in_range, layer_out, previous)
        outputs = lax.dynamic_update_index_in_dim(outputs, written[None, None], clipped, 1)
        if tick_index + 1 < tick_count:
            received = passed_along(layer_out, "section", 1)
    return outputs


def solution(mesh):
    placed = (
        P("group", "expert", None),
        P("section", "group", None, None),
        P("section", None),
        P("section", None, None),
        P("section", "expert", None, None),
        P("section", "expert", None, None),
    )
    return jax.shard_map(
        local,
        mesh=mesh,
        in_specs=placed,
        out_specs=P("section", "group", "expert", None),
        check_vma=False,
    )
```

profile of v0, /device:TPU:1, one launch (start us, length us, event | category | flops | bytes accessed | tf_op | source)
XLA Modules:
  0.0 350.2 jit_solution(10293664403971941060)
XLA Ops:
  0.0 0.8 broadcast_compare_fusion
  0.9 1.3 fusion.130
  2.2 0.8 bitcast_subtract_fusion
  3.0 1.1 fusion.34
  4.4 1.2 convolution_convert_fusion.2
  6.0 52.1 %all_to_all.30 = bf16[64,2,2048]{2,1,0:T(2,128)(2,1)S(1)} all-to-all(bf16[64,2,2048]{2,1,0:T(2,128)(2,1)S(1)} %bitcast.184), channel_id=1, replica_groups=mesh['section'=2,'group'=8,'expert'=64] {'expert'}, dimensions={0} | all-to-all | bytes 1048576 | tf_op jit(solution)/shard_map/all_to_all | solution.py:47
  58.3 3.1 fusion.46
  61.5 3.0 fusion.4
  64.5 1.8 copy.46
  66.3 8.5 %all-to-all-start.1 = ((f32[64,2,2048]{2,1,0:T(2,128)}), f32[64,2,2048]{2,1,0:T(2,128)S(1)}, u32[]{:S(2)}, u32[]{:S(2)}) async-start(f32[64,2,2048]{2,1,0:T(2,128)} %copy.46), calls=%async_computation.1 | async-start | bytes 2097152 | tf_op jit(solution)/shard_map/all_to_all | solution.py:56
  75.4 49.3 %all-to-all-done.1 = f32[64,2,2048]{2,1,0:T(2,128)S(1)} async-done(((f32[64,2,2048]{2,1,0:T(2,128)}), f32[64,2,2048]{2,1,0:T(2,128)S(1)}, u32[]{:S(2)}, u32[]{:S(2)}) %all-to-all-start.1) | async-done | bytes 1048608 | tf_op jit(solution)/shard_map/all_to_all | solution.py:56
  125.2 0.6 bitcast_dynamic-update-slice_fusion.1
  125.9 1.3 collective-permute-start
  127.2 1.3 fusion.132
  128.8 4.3 %collective-permute-done = bf16[64,2048]{1,0:T(8,128)(2,1)S(1)} collective-permute-done((bf16[64,2048]{1,0:T(8,128)(2,1)S(1)}, bf16[64,2048]{1,0:T(8,128)(2,1)S(1)}, u32[]{:S(2)}, u32[]{:S(2)}) %collective-permute-start) | collective-permute-done | bytes 262176 | tf_op jit(solution)/shard_map/ppermute | solution.py:10
  133.9 35.7 %all_to_all.31 = bf16[64,2,2048]{2,1,0:T(2,128)(2,1)S(1)} all-to-all(bf16[64,2,2048]{2,1,0:T(2,128)(2,1)S(1)} %bitcast.185), channel_id=1, replica_groups=mesh['section'=2,'group'=8,'expert'=64] {'expert'}, dimensions={0} | all-to-all | bytes 1048576 | tf_op jit(solution)/shard_map/all_to_all | solution.py:47
  169.9 3.1 fusion.61
  173.1 2.9 fusion.2
  176.0 1.8 copy.52
  177.8 8.9 %all-to-all-start.3 = ((f32[64,2,2048]{2,1,0:T(2,128)}), f32[64,2,2048]{2,1,0:T(2,128)S(1)}, u32[]{:S(2)}, u32[]{:S(2)}) async-start(f32[64,2,2048]{2,1,0:T(2,128)} %copy.52), calls=%async_computation.3 | async-start | bytes 2097152 | tf_op jit(solution)/shard_map/all_to_all | solution.py:56
  187.2 49.3 %all-to-all-done.3 = f32[64,2,2048]{2,1,0:T(2,128)S(1)} async-done(((f32[64,2,2048]{2,1,0:T(2,128)}), f32[64,2,2048]{2,1,0:T(2,128)S(1)}, u32[]{:S(2)}, u32[]{:S(2)}) %all-to-all-start.3) | async-done | bytes 1048608 | tf_op jit(solution)/shard_map/all_to_all | solution.py:56
  237.0 0.7 bitcast_dynamic-update-slice_fusion
  237.7 1.3 collective-permute-start.1
  239.0 1.3 fusion.134
  240.6 4.3 %collective-permute-done.1 = bf16[64,2048]{1,0:T(8,128)(2,1)S(1)} collective-permute-done((bf16[64,2048]{1,0:T(8,128)(2,1)S(1)}, bf16[64,2048]{1,0:T(8,128)(2,1)S(1)}, u32[]{:S(2)}, u32[]{:S(2)}) %collective-permute-start.1) | collective-permute-done | bytes 262176 | tf_op jit(solution)/shard_map/ppermute | solution.py:10
  245.8 36.1 %all_to_all.32 = bf16[64,2,2048]{2,1,0:T(2,128)(2,1)S(1)} all-to-all(bf16[64,2,2048]{2,1,0:T(2,128)(2,1)S(1)} %bitcast.186), channel_id=1, replica_groups=mesh['section'=2,'group'=8,'expert'=64] {'expert'}, dimensions={0} | all-to-all | bytes 1048576 | tf_op jit(solution)/shard_map/all_to_all | solution.py:47
  282.0 3.1 fusion.76
  285.2 2.9 fusion
  288.2 1.8 copy.58
  290.0 8.5 %all-to-all-start.5 = ((f32[64,2,2048]{2,1,0:T(2,128)}), f32[64,2,2048]{2,1,0:T(2,128)S(1)}, u32[]{:S(2)}, u32[]{:S(2)}) async-start(f32[64,2,2048]{2,1,0:T(2,128)} %copy.58), calls=%async_computation.5 | async-start | bytes 2097152 | tf_op jit(solution)/shard_map/all_to_all | solution.py:56
  299.0 49.4 %all-to-all-done.5 = f32[64,2,2048]{2,1,0:T(2,128)S(1)} async-done(((f32[64,2,2048]{2,1,0:T(2,128)}), f32[64,2,2048]{2,1,0:T(2,128)S(1)}, u32[]{:S(2)}, u32[]{:S(2)}) %all-to-all-start.5) | async-done | bytes 1048608 | tf_op jit(solution)/shard_map/all_to_all | solution.py:56
  348.8 1.4 fusion.20
  (51 shorter events, 7.0 us)
Async XLA Ops:
  0.0 74.9 %copy-start = (bf16[1,2048,8]{1,2,0:T(8,128)(2,1)S(1)}, bf16[1,2048,8]{1,2,0:T(8,128)(2,1)}, u32[]{:S(2)}) copy-start(bf16[1,2048,8]{1,2,0:T(8,128)(2,1)} %param.9) | copy-start | bytes 98308
  61.5 13.4 %copy-start.2 = (bf16[2,64,2048]{2,1,0:T(8,128)(2,1)S(1)}, bf16[2,64,2048]{2,1,0:T(8,128)(2,1)}, u32[]{:S(2)}) copy-start(bf16[2,64,2048]{2,1,0:T(8,128)(2,1)} %param.6) | copy-start | bytes 1572868
  61.5 13.4 %copy-start.3 = (f32[1,2048]{1,0:T(1,128)S(1)}, f32[1,2048]{1,0:T(1,128)}, u32[]{:S(2)}) copy-start(f32[1,2048]{1,0:T(1,128)} %param.8) | copy-start | bytes 24580
  66.3 58.4 %all-to-all-start.1 = ((f32[64,2,2048]{2,1,0:T(2,128)}), f32[64,2,2048]{2,1,0:T(2,128)S(1)}, u32[]{:S(2)}, u32[]{:S(2)}) async-start(f32[64,2,2048]{2,1,0:T(2,128)} %copy.46), calls=%async_computation.1 | async-start | bytes 2097152 | tf_op jit(solution)/shard_map/all_to_all | solution.py:56
  125.9 7.2 %collective-permute-start = (bf16[64,2048]{1,0:T(8,128)(2,1)S(1)}, bf16[64,2048]{1,0:T(8,128)(2,1)S(1)}, u32[]{:S(2)}, u32[]{:S(2)}) collective-permute-start(bf16[64,2048]{1,0:T(8,128)(2,1)S(1)} %get-tuple-element.25), channel_id=1, source_target_pairs={{0,512},{1,513},{2,514},{3,515},{4,516},{5,517},{6,518},{7,519},{8... | collective-permute-start | bytes 786440 | tf_op jit(solution)/shard_map/ppermute | solution.py:10
  177.8 58.8 %all-to-all-start.3 = ((f32[64,2,2048]{2,1,0:T(2,128)}), f32[64,2,2048]{2,1,0:T(2,128)S(1)}, u32[]{:S(2)}, u32[]{:S(2)}) async-start(f32[64,2,2048]{2,1,0:T(2,128)} %copy.52), calls=%async_computation.3 | async-start | bytes 2097152 | tf_op jit(solution)/shard_map/all_to_all | solution.py:56
  237.7 60.8 %copy-start.1 = (bf16[1,2,64,2048]{3,2,1,0:T(8,128)(2,1)}, bf16[1,2,64,2048]{3,2,1,0:T(8,128)(2,1)S(1)}, u32[]{:S(2)}) copy-start(bf16[1,2,64,2048]{3,2,1,0:T(8,128)(2,1)S(1)} %get-tuple-element.28) | copy-start | bytes 1572868
  237.7 7.2 %collective-permute-start.1 = (bf16[64,2048]{1,0:T(8,128)(2,1)S(1)}, bf16[64,2048]{1,0:T(8,128)(2,1)S(1)}, u32[]{:S(2)}, u32[]{:S(2)}) collective-permute-start(bf16[64,2048]{1,0:T(8,128)(2,1)S(1)} %get-tuple-element.29), channel_id=1, source_target_pairs={{0,512},{1,513},{2,514},{3,515},{4,516},{5,517},{6,518},{7,519},{8... | collective-permute-start | bytes 786440 | tf_op jit(solution)/shard_map/ppermute | solution.py:10
  290.0 58.4 %all-to-all-start.5 = ((f32[64,2,2048]{2,1,0:T(2,128)}), f32[64,2,2048]{2,1,0:T(2,128)S(1)}, u32[]{:S(2)}, u32[]{:S(2)}) async-start(f32[64,2,2048]{2,1,0:T(2,128)} %copy.58), calls=%async_computation.5 | async-start | bytes 2097152 | tf_op jit(solution)/shard_map/all_to_all | solution.py:56
where the time goes:
time: 354 us; the launch traced here: 350 us
  waiting for transfers between devices  157 us (44%)
  blocking collectives  124 us (35%)
  starting transfers between devices  28.5 us (8%)
  matrix products  24.6 us (7%)
  other arithmetic  8.33 us (2%)
  local copies, waits for them, and re-layouts  7.97 us (2%)
    all_to_all x3, waiting for transfers between devices, moe_layer(): lax.all_to_all(partial_value, 'expert', split_axis=0, concat_axis=0, tile...  148 us
    all_to_all x3, blocking collectives, moe_layer(): lax.all_to_all(outgoing, 'expert', split_axis=0, concat_axis=0, tiled=True)  124 us
    all_to_all x3, starting transfers between devices, moe_layer(): lax.all_to_all(partial_value, 'expert', split_axis=0, concat_axis=0, tile...  25.9 us
    dot_general x3, matrix products, moe_layer(): jnp.dot(flat_rows, w_first, preferred_element_type=jnp.float32)  9.29 us
    dot_general x3, matrix products, moe_layer(): jnp.dot(hidden, w_second, preferred_element_type=jnp.float32)  8.75 us
    ppermute x2, waiting for transfers between devices, passed_along(): lax.ppermute(value, axis, [(source, source + steps) for source in range(l...  8.59 us
  transfers between devices with their start and end apart: 5, of which 5 were waited for; matrix products, arithmetic and copies ran while one was open for 1% of the time, Pallas kernels for 0%

commit v1 on v0

v1 whole, which is shorter than its diff:
```python
import jax
import jax.numpy as jnp
from jax import lax
from jax.sharding import PartitionSpec as P

SWAP = [(0, 1), (1, 0)]


def layer(current, picks, gain_row, router_cols, own, other, use_own, device, owners, shards_each):
    tok_rows, width = current.shape
    experts, capacity = picks.shape
    slots = 2 * capacity // owners
    floats = current.astype(jnp.float32)
    inverse_rms = lax.rsqrt(jnp.mean(floats * floats, axis=-1, keepdims=True) + 1e-06)
    normed = (floats * inverse_rms * gain_row).astype(jnp.bfloat16)
    gate_all = jax.nn.sigmoid(jnp.dot(normed, router_cols, preferred_element_type=jnp.float32))
    local_idx = picks - device * tok_rows
    tok_hit = local_idx[:, :, None] == jnp.arange(tok_rows, dtype=jnp.int32)[None, None, :]
    chosen_here = tok_hit.any(axis=1).astype(jnp.int32)
    rank = jnp.cumsum(chosen_here, axis=1) - 1
    selector = (
        (rank[:, None, :] == jnp.arange(slots, dtype=jnp.int32)[None, :, None])
        & (chosen_here[:, None, :] > 0)
    ).astype(jnp.float32)
    flat_select = selector.reshape(experts * slots, tok_rows)
    gate_slot = jnp.einsum("xst,tx->xs", selector, gate_all, precision=lax.Precision.HIGHEST)
    dispatched = jnp.dot(
        flat_select.astype(jnp.bfloat16), normed, preferred_element_type=jnp.float32
    ).astype(jnp.bfloat16)
    outgoing = jnp.broadcast_to(
        dispatched.reshape(experts, 1, slots, width), (experts, shards_each, slots, width)
    ).reshape(owners, slots, width)
    arrived = lax.all_to_all(outgoing, "expert", split_axis=0, concat_axis=0, tiled=True)

    def ffn(rows, first, second):
        hidden = jax.nn.gelu(
            jnp.dot(rows, first, preferred_element_type=jnp.float32), approximate=True
        ).astype(jnp.bfloat16)
        return jnp.dot(hidden, second, preferred_element_type=jnp.float32).astype(jnp.bfloat16)

    rows = arrived.reshape(-1, width)
    partial_value = lax.cond(
        use_own,
        lambda r, a, b: ffn(r, *a),
        lambda r, a, b: ffn(r, *b),
        rows,
        own,
        other,
    ).reshape(owners, slots, width)
    returned = lax.all_to_all(partial_value, "expert", split_axis=0, concat_axis=0, tiled=True)
    summed = (
        returned.reshape(experts, shards_each, slots, width).astype(jnp.float32).sum(axis=1)
    )
    weighted = summed * gate_slot[:, :, None]
    contrib = jnp.dot(
        flat_select.T, weighted.reshape(experts * slots, width), precision=lax.Precision.HIGHEST
    )
    return (floats + contrib).astype(jnp.bfloat16)


def local(tokens, chosen, norm_gain, router, w_in, w_out):
    owners = lax.axis_size("expert")
    core = lax.axis_index("section")
    device = lax.axis_index("expert")
    experts = chosen.shape[2]
    shards_each = owners // experts

    def swap(value):
        return lax.ppermute(value, "section", SWAP)

    first = core == 0
    own = (w_in[0, 0], w_out[0, 0])
    other = (swap(own[0]), swap(own[1]))
    small_other = (swap(chosen[0]), swap(norm_gain[0]), swap(router[0]))
    small_own = (chosen[0], norm_gain[0], router[0])
    current = lax.dynamic_index_in_dim(tokens, core, 0, keepdims=False)
    results = []
    for section in range(2):
        use_own = core == section
        picks, gain_row, router_cols = (
            jnp.where(use_own, a, b) for a, b in zip(small_own, small_other)
        )
        picks = lax.dynamic_index_in_dim(picks, core, 0, keepdims=False)
        current = layer(
            current, picks, gain_row, router_cols, own, other, use_own, device, owners, shards_each
        )
        results.append(current)
    got = swap(jnp.where(first, results[1], results[0]))
    return jnp.where(
        first, jnp.stack([results[0], got]), jnp.stack([got, results[1]])
    )[None]


def solution(mesh):
    placed = (
        P("group", "expert", None),
        P("section", "group", None, None),
        P("section", None),
        P("section", None, None),
        P("section", "expert", None, None),
        P("section", "expert", None, None),
    )
    return jax.shard_map(
        local,
        mesh=mesh,
        in_specs=placed,
        out_specs=P("section", "group", "expert", None),
        check_vma=False,
    )
```

time: 354 us -> 211 us (0.60)
  blocking collectives: 124 us -> 0 us
  starting transfers between devices: 28.5 us -> 65.5 us
  waiting for transfers between devices: 157 us -> 120 us
  matrix products: 24.6 us -> 13.2 us
    all_to_all x3 -> x0, blocking collectives: 124 us -> none  [moe_layer(): lax.all_to_all(outgoing, 'expert', split_axis=0, concat_axis=0, tiled=True)]
    all_to_all x3 -> x4, waiting for transfers between devices: 148 us -> 113 us  [the longest x2 59.1 us: layer(): lax.all_to_all(outgoing, 'expert', split_axis=0, concat_axis=0, tiled=True)]
    ppermute x2 -> x6, starting transfers between devices: 2.58 us -> 30.8 us  [swap(): return lax.ppermute(value, 'section', SWAP)]
    dot_general x21 -> x10, matrix products: 24.6 us -> 13.2 us  [the longest x2 9.92 us: ffn(): jnp.dot(hidden, second, preferred_element_type=jnp.float32)]
    all_to_all x3 -> x4, starting transfers between devices: 25.9 us -> 34.7 us  [the longest x2 17.8 us: layer(): lax.all_to_all(outgoing, 'expert', split_axis=0, concat_axis=0, tiled=True)]
    dot_general x6 -> x0, local copies, waits for them, and re-layouts: 5.71 us -> none  [moe_layer(): jnp.dot(hidden, w_second, preferred_element_type=jnp.float32)]
    ppermute x2 -> x6, waiting for transfers between devices: 8.59 us -> 7.32 us  [swap(): return lax.ppermute(value, 'section', SWAP)]
  transfers between devices with their start and end apart: 5 -> 10, of which waited for: 5 -> 7; matrix products, arithmetic and copies ran while one was open for 1% -> 3% of each run, Pallas kernels for 0% -> 0%
where the time goes in v1:
time: 211 us; the launch traced here: 210 us
  waiting for transfers between devices  120 us (57%)
  starting transfers between devices  65.5 us (31%)
  matrix products  13.2 us (6%)
  other arithmetic  5.18 us (2%)
  local copies, waits for them, and re-layouts  5.14 us (2%)
    all_to_all x2, waiting for transfers between devices, layer(): lax.all_to_all(outgoing, 'expert', split_axis=0, concat_axis=0, tiled=True)  59.1 us
    all_to_all x2, waiting for transfers between devices, layer(): lax.all_to_all(partial_value, 'expert', split_axis=0, concat_axis=0, tile...  53.8 us
    ppermute x6, starting transfers between devices, swap(): return lax.ppermute(value, 'section', SWAP)  30.8 us
    all_to_all x2, starting transfers between devices, layer(): lax.all_to_all(outgoing, 'expert', split_axis=0, concat_axis=0, tiled=True)  17.8 us
    all_to_all x2, starting transfers between devices, layer(): lax.all_to_all(partial_value, 'expert', split_axis=0, concat_axis=0, tile...  16.9 us
    dot_general x2, matrix products, ffn(): jnp.dot(hidden, second, preferred_element_type=jnp.float32)  9.92 us
    ppermute x6, waiting for transfers between devices, swap(): return lax.ppermute(value, 'section', SWAP)  7.32 us
  transfers between devices with their start and end apart: 10, of which 7 were waited for; matrix products, arithmetic and copies ran while one was open for 3% of the time, Pallas kernels for 0%

profile of v1, /device:TPU:1, one launch (start us, length us, event | category | flops | bytes accessed | tf_op | source)
XLA Modules:
  0.0 209.8 jit_solution(10289689765691733070)
XLA Ops:
  0.0 16.0 %collective-permute-start.2 = (bf16[2048,1024]{1,0:T(8,128)(2,1)}, bf16[2048,1024]{1,0:T(8,128)(2,1)}, u32[]{:S(2)}, u32[]{:S(2)}) collective-permute-start(bf16[2048,1024]{1,0:T(8,128)(2,1)} %bitcast.87), channel_id=1, source_target_pairs={{0,512},{512,0},{1,513},{513,1},{2,514},{514,2},{3,515},{515,3},{4... | collective-permute-start | bytes 12582920 | tf_op jit(solution)/shard_map/ppermute | solution.py:69
  16.0 1.9 collective-permute-start.3
  18.0 2.4 %collective-permute-start = (s32[2,8,64]{2,1,0:T(8,128)}, s32[2,8,64]{2,1,0:T(8,128)S(1)}, u32[]{:S(2)}, u32[]{:S(2)}) collective-permute-start(s32[2,8,64]{2,1,0:T(8,128)} %bitcast.102), channel_id=1, source_target_pairs={{0,512},{512,0},{1,513},{513,1},{2,514},{514,2},{3,515},{515,3},{4... | collective-permute-start | bytes 12296 | tf_op jit(solution)/shard_map/ppermute | solution.py:69
  20.4 1.9 collective-permute-start.1
  22.3 1.1 fusion.84
  23.4 5.7 %collective-permute-done = s32[2,8,64]{2,1,0:T(8,128)S(1)} collective-permute-done((s32[2,8,64]{2,1,0:T(8,128)}, s32[2,8,64]{2,1,0:T(8,128)S(1)}, u32[]{:S(2)}, u32[]{:S(2)}) %collective-permute-start) | collective-permute-done | bytes 4128 | tf_op jit(solution)/shard_map/ppermute | solution.py:69
  29.1 0.7 subtract_bitcast_fusion
  30.3 0.7 broadcast_select_fusion.1
  31.0 1.2 convolution_convert_fusion.1
  32.3 1.1 broadcast_in_dim.9
  33.4 9.3 %all-to-all-start = ((bf16[64,2,2048]{2,1,0:T(2,128)(2,1)}), bf16[64,2,2048]{2,1,0:T(2,128)(2,1)S(1)}, u32[]{:S(2)}, u32[]{:S(2)}) async-start(bf16[64,2,2048]{2,1,0:T(2,128)(2,1)} %bitcast.6), calls=%async_computation | async-start | bytes 1048576 | tf_op jit(solution)/shard_map/all_to_all | solution.py:33
  42.7 29.8 %all-to-all-done = bf16[64,2,2048]{2,1,0:T(2,128)(2,1)S(1)} async-done(((bf16[64,2,2048]{2,1,0:T(2,128)(2,1)}), bf16[64,2,2048]{2,1,0:T(2,128)(2,1)S(1)}, u32[]{:S(2)}, u32[]{:S(2)}) %all-to-all-start) | async-done | bytes 524320 | tf_op jit(solution)/shard_map/all_to_all | solution.py:33
  72.7 5.0 %conditional.4 = (bf16[128,2048]{1,0:T(8,128)(2,1)S(1)}) conditional(s32[]{:T(128)} %convert_element_type.130, (bf16[128,2048]{1,0:T(8,128)(2,1)S(1)}, bf16[2048,1024]{1,0:T(8,128)(2,1)}, bf16[1024,2048]{1,0:T(8,128)(2,1)}) %tuple.23, (bf16[128,2048]{1,0:T(8,128)(2,1)S(1)}, bf16[2048,1024]{1,0:T(8,128)(2,1)}, bf16[1024,2048]{1,0:T(8,128)(2,1)}) %tuple.41), branch_computations={%region_3.4_spmd, %region_4.5_spmd} | conditional | flops 1074921472 | bytes 9437192
  72.7 5.0 %fusion.8 = bf16[128,2048]{1,0:T(8,128)(2,1)S(1)} fusion(bf16[1024,2048]{1,0:T(8,128)(2,1)} %get-tuple-element.41, bf16[128,2048]{1,0:T(8,128)(2,1)S(1)} %get-tuple-element.39, bf16[2048,1024]{1,0:T(8,128)(2,1)} %get-tuple-element.40), kind=kOutput, calls=%fused_computation.9 | convolution fusion | flops 1074921472 | bytes 9437184 | tf_op jit(solution)/shard_map/cond/branch_0_fun/dot_general | solution.py:39
  77.7 1.1 reshape.210
  78.9 8.3 %all-to-all-start.1 = ((bf16[64,2,2048]{2,1,0:T(2,128)(2,1)}), bf16[64,2,2048]{2,1,0:T(2,128)(2,1)S(1)}, u32[]{:S(2)}, u32[]{:S(2)}) async-start(bf16[64,2,2048]{2,1,0:T(2,128)(2,1)} %reshape.210), calls=%async_computation.1 | async-start | bytes 1048576 | tf_op jit(solution)/shard_map/all_to_all | solution.py:50
  87.2 3.4 %collective-permute-start.4 = (bf16[2048,8]{0,1:T(8,128)(2,1)S(1)}, bf16[2048,8]{0,1:T(8,128)(2,1)S(1)}, u32[]{:S(2)}, u32[]{:S(2)}) collective-permute-start(bf16[2048,8]{0,1:T(8,128)(2,1)S(1)} %bitcast.104), channel_id=1, source_target_pairs={{0,512},{512,0},{1,513},{513,1},{2,514},{514,2},{3,515},{515,3},{4... | collective-permute-start | bytes 98312 | tf_op jit(solution)/shard_map/ppermute | solution.py:69
  90.9 0.5 collective-permute-done.4
  91.8 24.9 %all-to-all-done.1 = bf16[64,2,2048]{2,1,0:T(2,128)(2,1)S(1)} async-done(((bf16[64,2,2048]{2,1,0:T(2,128)(2,1)}), bf16[64,2,2048]{2,1,0:T(2,128)(2,1)S(1)}, u32[]{:S(2)}, u32[]{:S(2)}) %all-to-all-start.1) | async-done | bytes 524320 | tf_op jit(solution)/shard_map/all_to_all | solution.py:50
  117.3 0.5 fusion.89
  118.1 1.1 broadcast_in_dim.11
  119.3 8.4 %all-to-all-start.2 = ((bf16[64,2,2048]{2,1,0:T(2,128)(2,1)}), bf16[64,2,2048]{2,1,0:T(2,128)(2,1)S(1)}, u32[]{:S(2)}, u32[]{:S(2)}) async-start(bf16[64,2,2048]{2,1,0:T(2,128)(2,1)} %bitcast.19), calls=%async_computation.2 | async-start | bytes 1048576 | tf_op jit(solution)/shard_map/all_to_all | solution.py:33
  127.7 29.4 %all-to-all-done.2 = bf16[64,2,2048]{2,1,0:T(2,128)(2,1)S(1)} async-done(((bf16[64,2,2048]{2,1,0:T(2,128)(2,1)}), bf16[64,2,2048]{2,1,0:T(2,128)(2,1)S(1)}, u32[]{:S(2)}, u32[]{:S(2)}) %all-to-all-start.2) | async-done | bytes 524320 | tf_op jit(solution)/shard_map/all_to_all | solution.py:33
  157.3 5.1 %conditional.5 = (bf16[128,2048]{1,0:T(8,128)(2,1)S(1)}) conditional(s32[]{:T(128)} %convert_element_type.145, (bf16[128,2048]{1,0:T(8,128)(2,1)S(1)}, bf16[2048,1024]{1,0:T(8,128)(2,1)}, bf16[1024,2048]{1,0:T(8,128)(2,1)}) %tuple.25, (bf16[128,2048]{1,0:T(8,128)(2,1)S(1)}, bf16[2048,1024]{1,0:T(8,128)(2,1)}, bf16[1024,2048]{1,0:T(8,128)(2,1)}) %tuple.42), branch_computations={%region_9.10_spmd, %region_10.11_spmd} | conditional | flops 1074921472 | bytes 9437192
  157.5 4.9 %fusion.62 = bf16[128,2048]{1,0:T(8,128)(2,1)S(1)} fusion(bf16[1024,2048]{1,0:T(8,128)(2,1)} %get-tuple-element.50, bf16[128,2048]{1,0:T(8,128)(2,1)S(1)} %get-tuple-element.48, bf16[2048,1024]{1,0:T(8,128)(2,1)} %get-tuple-element.49), kind=kOutput, calls=%fused_computation.63 | convolution fusion | flops 1074921472 | bytes 9437184 | tf_op jit(solution)/shard_map/cond/branch_1_fun/dot_general | solution.py:39
  162.4 1.1 reshape.213
  163.6 8.6 %all-to-all-start.3 = ((bf16[64,2,2048]{2,1,0:T(2,128)(2,1)}), bf16[64,2,2048]{2,1,0:T(2,128)(2,1)S(1)}, u32[]{:S(2)}, u32[]{:S(2)}) async-start(bf16[64,2,2048]{2,1,0:T(2,128)(2,1)} %reshape.213), calls=%async_computation.3 | async-start | bytes 1048576 | tf_op jit(solution)/shard_map/all_to_all | solution.py:50
  172.6 28.9 %all-to-all-done.3 = bf16[64,2,2048]{2,1,0:T(2,128)(2,1)S(1)} async-done(((bf16[64,2,2048]{2,1,0:T(2,128)(2,1)}), bf16[64,2,2048]{2,1,0:T(2,128)(2,1)S(1)}, u32[]{:S(2)}, u32[]{:S(2)}) %all-to-all-start.3) | async-done | bytes 524320 | tf_op jit(solution)/shard_map/all_to_all | solution.py:50
  202.1 0.5 broadcast_select_fusion
  202.5 5.2 %collective-permute-start.5 = (bf16[64,2048]{1,0:T(8,128)(2,1)S(1)}, bf16[64,2048]{1,0:T(8,128)(2,1)S(1)}, u32[]{:S(2)}, u32[]{:S(2)}) collective-permute-start(bf16[64,2048]{1,0:T(8,128)(2,1)S(1)} %get-tuple-element.63), channel_id=1, source_target_pairs={{0,512},{512,0},{1,513},{513,1},{2,514},{514,2},{3,515},{515,3},{4... | collective-permute-start | bytes 786440 | tf_op jit(solution)/shard_map/ppermute | solution.py:69
  207.7 1.1 collective-permute-done.5
  208.9 0.9 maximum_select_fusion
  (36 shorter events, 3.5 us)
Async XLA Ops:
  0.0 72.7 %collective-permute-start.2 = (bf16[2048,1024]{1,0:T(8,128)(2,1)}, bf16[2048,1024]{1,0:T(8,128)(2,1)}, u32[]{:S(2)}, u32[]{:S(2)}) collective-permute-start(bf16[2048,1024]{1,0:T(8,128)(2,1)} %bitcast.87), channel_id=1, source_target_pairs={{0,512},{512,0},{1,513},{513,1},{2,514},{514,2},{3,515},{515,3},{4... | collective-permute-start | bytes 12582920 | tf_op jit(solution)/shard_map/ppermute | solution.py:69
  16.0 56.7 %collective-permute-start.3 = (bf16[1024,2048]{1,0:T(8,128)(2,1)}, bf16[1024,2048]{1,0:T(8,128)(2,1)}, u32[]{:S(2)}, u32[]{:S(2)}) collective-permute-start(bf16[1024,2048]{1,0:T(8,128)(2,1)} %bitcast.90), channel_id=1, source_target_pairs={{0,512},{512,0},{1,513},{513,1},{2,514},{514,2},{3,515},{515,3},{4... | collective-permute-start | bytes 12582920 | tf_op jit(solution)/shard_map/ppermute | solution.py:69
  18.0 11.2 %collective-permute-start = (s32[2,8,64]{2,1,0:T(8,128)}, s32[2,8,64]{2,1,0:T(8,128)S(1)}, u32[]{:S(2)}, u32[]{:S(2)}) collective-permute-start(s32[2,8,64]{2,1,0:T(8,128)} %bitcast.102), channel_id=1, source_target_pairs={{0,512},{512,0},{1,513},{513,1},{2,514},{514,2},{3,515},{515,3},{4... | collective-permute-start | bytes 12296 | tf_op jit(solution)/shard_map/ppermute | solution.py:69
  20.4 9.9 %collective-permute-start.1 = (f32[2048]{0:T(1024)}, f32[2048]{0:T(1024)S(1)}, u32[]{:S(2)}, u32[]{:S(2)}) collective-permute-start(f32[2048]{0:T(1024)} %bitcast.97), channel_id=1, source_target_pairs={{0,512},{512,0},{1,513},{513,1},{2,514},{514,2},{3,515},{515,3},{4... | collective-permute-start | bytes 24584 | tf_op jit(solution)/shard_map/ppermute | solution.py:69
  33.4 39.1 %all-to-all-start = ((bf16[64,2,2048]{2,1,0:T(2,128)(2,1)}), bf16[64,2,2048]{2,1,0:T(2,128)(2,1)S(1)}, u32[]{:S(2)}, u32[]{:S(2)}) async-start(bf16[64,2,2048]{2,1,0:T(2,128)(2,1)} %bitcast.6), calls=%async_computation | async-start | bytes 1048576 | tf_op jit(solution)/shard_map/all_to_all | solution.py:33
  72.7 14.5 %copy-start.1 = (bf16[1,2048,8]{1,2,0:T(8,128)(2,1)S(1)}, bf16[1,2048,8]{1,2,0:T(8,128)(2,1)}, u32[]{:S(2)}) copy-start(bf16[1,2048,8]{1,2,0:T(8,128)(2,1)} %param.13) | copy-start | bytes 98308
  72.7 18.7 %copy-start = (bf16[2,64,2048]{2,1,0:T(8,128)(2,1)S(1)}, bf16[2,64,2048]{2,1,0:T(8,128)(2,1)}, u32[]{:S(2)}) copy-start(bf16[2,64,2048]{2,1,0:T(8,128)(2,1)} %param.10) | copy-start | bytes 1572868
  78.9 37.8 %all-to-all-start.1 = ((bf16[64,2,2048]{2,1,0:T(2,128)(2,1)}), bf16[64,2,2048]{2,1,0:T(2,128)(2,1)S(1)}, u32[]{:S(2)}, u32[]{:S(2)}) async-start(bf16[64,2,2048]{2,1,0:T(2,128)(2,1)} %reshape.210), calls=%async_computation.1 | async-start | bytes 1048576 | tf_op jit(solution)/shard_map/all_to_all | solution.py:50
  87.2 4.2 %collective-permute-start.4 = (bf16[2048,8]{0,1:T(8,128)(2,1)S(1)}, bf16[2048,8]{0,1:T(8,128)(2,1)S(1)}, u32[]{:S(2)}, u32[]{:S(2)}) collective-permute-start(bf16[2048,8]{0,1:T(8,128)(2,1)S(1)} %bitcast.104), channel_id=1, source_target_pairs={{0,512},{512,0},{1,513},{513,1},{2,514},{514,2},{3,515},{515,3},{4... | collective-permute-start | bytes 98312 | tf_op jit(solution)/shard_map/ppermute | solution.py:69
  119.3 37.8 %all-to-all-start.2 = ((bf16[64,2,2048]{2,1,0:T(2,128)(2,1)}), bf16[64,2,2048]{2,1,0:T(2,128)(2,1)S(1)}, u32[]{:S(2)}, u32[]{:S(2)}) async-start(bf16[64,2,2048]{2,1,0:T(2,128)(2,1)} %bitcast.19), calls=%async_computation.2 | async-start | bytes 1048576 | tf_op jit(solution)/shard_map/all_to_all | solution.py:33
  163.6 38.0 %all-to-all-start.3 = ((bf16[64,2,2048]{2,1,0:T(2,128)(2,1)}), bf16[64,2,2048]{2,1,0:T(2,128)(2,1)S(1)}, u32[]{:S(2)}, u32[]{:S(2)}) async-start(bf16[64,2,2048]{2,1,0:T(2,128)(2,1)} %reshape.213), calls=%async_computation.3 | async-start | bytes 1048576 | tf_op jit(solution)/shard_map/all_to_all | solution.py:50
  202.5 6.3 %collective-permute-start.5 = (bf16[64,2048]{1,0:T(8,128)(2,1)S(1)}, bf16[64,2048]{1,0:T(8,128)(2,1)S(1)}, u32[]{:S(2)}, u32[]{:S(2)}) collective-permute-start(bf16[64,2048]{1,0:T(8,128)(2,1)S(1)} %get-tuple-element.63), channel_id=1, source_target_pairs={{0,512},{512,0},{1,513},{513,1},{2,514},{514,2},{3,515},{515,3},{4... | collective-permute-start | bytes 786440 | tf_op jit(solution)/shard_map/ppermute | solution.py:69

commit v2 on v1

--- a/solution.py
+++ b/solution.py
@@ -1,9 +1,32 @@
 import jax
 import jax.numpy as jnp
 from jax import lax
+from jax.experimental import pallas as pl
+from jax.experimental.pallas import tpu as pltpu
 from jax.sharding import PartitionSpec as P
 
 SWAP = [(0, 1), (1, 0)]
+STAGGER_NS = 14000
+
+
+def hold_kernel(core_ref, value_ref, out_ref):
+    @pl.when(core_ref[0] == 1)
+    def _():
+        pl.delay(STAGGER_NS)
+
+    out_ref[...] = value_ref[...]
+
+
+def hold(value, core):
+    return pl.pallas_call(
+        hold_kernel,
+        out_shape=jax.ShapeDtypeStruct(value.shape, value.dtype),
+        in_specs=[
+            pl.BlockSpec(memory_space=pltpu.SMEM),
+            pl.BlockSpec(memory_space=pltpu.VMEM),
+        ],
+        out_specs=pl.BlockSpec(memory_space=pltpu.VMEM),
+    )(core.reshape(1), value)
 
 
 def layer(current, picks, gain_row, router_cols, own, other, use_own, device, owners, shards_each):
@@ -32,18 +55,18 @@
     ).reshape(owners, slots, width)
     arrived = lax.all_to_all(outgoing, "expert", split_axis=0, concat_axis=0, tiled=True)
 
+
     def ffn(rows, first, second):
         hidden = jax.nn.gelu(
             jnp.dot(rows, first, preferred_element_type=jnp.float32), approximate=True
         ).astype(jnp.bfloat16)
         return jnp.dot(hidden, second, preferred_element_type=jnp.float32).astype(jnp.bfloat16)
 
-    rows = arrived.reshape(-1, width)
     partial_value = lax.cond(
         use_own,
         lambda r, a, b: ffn(r, *a),
         lambda r, a, b: ffn(r, *b),
-        rows,
+        arrived.reshape(-1, width),
         own,
         other,
     ).reshape(owners, slots, width)
@@ -69,20 +92,40 @@
         return lax.ppermute(value, "section", SWAP)
 
     first = core == 0
+    micro, capacity = chosen.shape[1], chosen.shape[3]
+    width = tokens.shape[2]
+    packed = jnp.concatenate(
+        [
+            norm_gain,
+            router[0].astype(jnp.float32).T,
+            jnp.pad(chosen[0].astype(jnp.float32).reshape(1, -1), ((0, 0), (0, -chosen.size % width))),
+        ]
+    )
+    packed_other = swap(packed)
     own = (w_in[0, 0], w_out[0, 0])
     other = (swap(own[0]), swap(own[1]))
-    small_other = (swap(chosen[0]), swap(norm_gain[0]), swap(router[0]))
-    small_own = (chosen[0], norm_gain[0], router[0])
     current = lax.dynamic_index_in_dim(tokens, core, 0, keepdims=False)
     results = []
     for section in range(2):
         use_own = core == section
-        picks, gain_row, router_cols = (
-            jnp.where(use_own, a, b) for a, b in zip(small_own, small_other)
-        )
+        small = jnp.where(use_own, packed, packed_other)
+        gain_row = small[:1]
+        router_cols = small[1 : 1 + experts].astype(jnp.bfloat16).T
+        picks = small[1 + experts, : chosen.size].astype(jnp.int32).reshape(micro, experts, capacity)
         picks = lax.dynamic_index_in_dim(picks, core, 0, keepdims=False)
+        if section == 0:
+            picks = hold(picks, core)
         current = layer(
-            current, picks, gain_row, router_cols, own, other, use_own, device, owners, shards_each
+            current,
+            picks,
+            gain_row,
+            router_cols,
+            own,
+            other,
+            use_own,
+            device,
+            owners,
+            shards_each,
         )
         results.append(current)
     got = swap(jnp.where(first, results[1], results[0]))

time: 211 us -> 182 us (0.86)
  waiting for transfers between devices: 120 us -> 87.9 us
  Pallas kernels: 0 us -> 15.3 us
  starting transfers between devices: 65.5 us -> 51.2 us
  other arithmetic: 5.18 us -> 7.52 us
    all_to_all x2, waiting for transfers between devices: 59.1 us -> 42.1 us  [layer(): lax.all_to_all(outgoing, 'expert', split_axis=0, concat_axis=0, tiled=True)]
    pallas_call x0 -> x1, Pallas kernels: none -> 15.3 us  [hold(): pl.pallas_call(hold_kernel, out_shape=jax.ShapeDtypeStruct(value.shape, v...]
    all_to_all x2, waiting for transfers between devices: 53.8 us -> 44.3 us  [layer(): lax.all_to_all(partial_value, 'expert', split_axis=0, concat_axis=0, tile...]
    ppermute x6 -> x4, starting transfers between devices: 30.8 us -> 22.3 us  [swap(): return lax.ppermute(value, 'section', SWAP)]
    ppermute x6 -> x4, waiting for transfers between devices: 7.32 us -> 1.51 us  [swap(): return lax.ppermute(value, 'section', SWAP)]
    all_to_all x2, starting transfers between devices: 16.9 us -> 13.5 us  [layer(): lax.all_to_all(partial_value, 'expert', split_axis=0, concat_axis=0, tile...]
    all_to_all x2, starting transfers between devices: 17.8 us -> 15.4 us  [layer(): lax.all_to_all(outgoing, 'expert', split_axis=0, concat_axis=0, tiled=True)]
  transfers between devices with their start and end apart: 10 -> 8, of which waited for: 7 -> 5; matrix products, arithmetic and copies ran while one was open for 3% -> 4% of each run, Pallas kernels for 0% -> 8%
where the time goes in v2:
time: 182 us
  waiting for transfers between devices  87.9 us (48%)
  starting transfers between devices  51.2 us (28%)
  Pallas kernels  15.3 us (8%)
  matrix products  13.3 us (7%)
  other arithmetic  7.52 us (4%)
  local copies, waits for them, and re-layouts  5.97 us (3%)
    all_to_all x2, waiting for transfers between devices, layer(): lax.all_to_all(partial_value, 'expert', split_axis=0, concat_axis=0, tile...  44.3 us
    all_to_all x2, waiting for transfers between devices, layer(): lax.all_to_all(outgoing, 'expert', split_axis=0, concat_axis=0, tiled=True)  42.1 us
    ppermute x4, starting transfers between devices, swap(): return lax.ppermute(value, 'section', SWAP)  22.3 us
    all_to_all x2, starting transfers between devices, layer(): lax.all_to_all(outgoing, 'expert', split_axis=0, concat_axis=0, tiled=True)  15.4 us
    pallas_call x1, Pallas kernels, hold(): pl.pallas_call(hold_kernel, out_shape=jax.ShapeDtypeStruct(value.shape, v...  15.3 us
    all_to_all x2, starting transfers between devices, layer(): lax.all_to_all(partial_value, 'expert', split_axis=0, concat_axis=0, tile...  13.5 us
    dot_general x2, matrix products, ffn(): jnp.dot(hidden, second, preferred_element_type=jnp.float32)  9.98 us
  transfers between devices with their start and end apart: 8, of which 5 were waited for; matrix products, arithmetic and copies ran while one was open for 4% of the time, Pallas kernels for 8%

profile of v2, /device:TPU:1, one launch (start us, length us, event | category | flops | bytes accessed | tf_op | source)
XLA Modules:
  0.0 181.6 jit_solution(17544018475552172061)
XLA Ops:
  0.0 0.7 convert_element_type.165
  0.8 0.8 convert_bitcast_fusion.1
  1.5 0.7 select_maximum_fusion
  2.3 16.0 %collective-permute-start = (f32[10,2048]{1,0:T(8,128)S(1)}, f32[10,2048]{1,0:T(8,128)S(1)}, u32[]{:S(2)}, u32[]{:S(2)}) collective-permute-start(f32[10,2048]{1,0:T(8,128)S(1)} %select_maximum_fusion), channel_id=1, source_target_pairs={{0,512},{512,0},{1,513},{513,1},{2,514},{514,2},{3,515},{515,3},{4... | collective-permute-start | bytes 245768 | tf_op jit(solution)/shard_map/ppermute | solution.py:92
  18.3 1.9 %collective-permute-start.1 = (bf16[2048,1024]{1,0:T(8,128)(2,1)}, bf16[2048,1024]{1,0:T(8,128)(2,1)}, u32[]{:S(2)}, u32[]{:S(2)}) collective-permute-start(bf16[2048,1024]{1,0:T(8,128)(2,1)} %bitcast.86), channel_id=1, source_target_pairs={{0,512},{512,0},{1,513},{513,1},{2,514},{514,2},{3,515},{515,3},{4... | collective-permute-start | bytes 12582920 | tf_op jit(solution)/shard_map/ppermute | solution.py:92
  20.2 2.4 %collective-permute-start.2 = (bf16[1024,2048]{1,0:T(8,128)(2,1)}, bf16[1024,2048]{1,0:T(8,128)(2,1)}, u32[]{:S(2)}, u32[]{:S(2)}) collective-permute-start(bf16[1024,2048]{1,0:T(8,128)(2,1)} %bitcast.89), channel_id=1, source_target_pairs={{0,512},{512,0},{1,513},{513,1},{2,514},{514,2},{3,515},{515,3},{4... | collective-permute-start | bytes 12582920 | tf_op jit(solution)/shard_map/ppermute | solution.py:92
  22.7 1.1 fusion.84
  23.8 0.7 broadcast_select_fusion.1
  24.7 0.6 dynamic-slice_bitcast_fusion.value_ref
  25.3 15.3 %shard_map.64 = s32[8,64]{1,0:T(8,128)} custom-call(s32[1]{0:T(128)} %bitcast.1.core_ref, s32[8,64]{1,0:T(8,128)} %dynamic-slice_bitcast_fusion.value_ref), custom_call_target="tpu_custom_call" | custom-call | tf_op jit(solution)/shard_map/pallas_call | solution.py:21
  40.5 0.7 broadcast_subtract_fusion
  41.6 1.2 convolution_convert_fusion.1
  42.9 1.1 broadcast_in_dim.9
  44.0 9.3 %all-to-all-start = ((bf16[64,2,2048]{2,1,0:T(2,128)(2,1)}), bf16[64,2,2048]{2,1,0:T(2,128)(2,1)S(1)}, u32[]{:S(2)}, u32[]{:S(2)}) async-start(bf16[64,2,2048]{2,1,0:T(2,128)(2,1)} %bitcast.8), calls=%async_computation | async-start | bytes 1048576 | tf_op jit(solution)/shard_map/all_to_all | solution.py:56
  53.3 20.6 %all-to-all-done = bf16[64,2,2048]{2,1,0:T(2,128)(2,1)S(1)} async-done(((bf16[64,2,2048]{2,1,0:T(2,128)(2,1)}), bf16[64,2,2048]{2,1,0:T(2,128)(2,1)S(1)}, u32[]{:S(2)}, u32[]{:S(2)}) %all-to-all-start) | async-done | bytes 524320 | tf_op jit(solution)/shard_map/all_to_all | solution.py:56
  74.2 5.0 %conditional.4 = (bf16[128,2048]{1,0:T(8,128)(2,1)S(1)}) conditional(s32[]{:T(128)} %convert_element_type.170, (bf16[128,2048]{1,0:T(8,128)(2,1)S(1)}, bf16[2048,1024]{1,0:T(8,128)(2,1)}, bf16[1024,2048]{1,0:T(8,128)(2,1)}) %tuple.23, (bf16[128,2048]{1,0:T(8,128)(2,1)S(1)}, bf16[2048,1024]{1,0:T(8,128)(2,1)}, bf16[1024,2048]{1,0:T(8,128)(2,1)}) %tuple.40), branch_computations={%region_3.4_spmd, %region_4.5_spmd} | conditional | flops 1074921472 | bytes 9437192
  74.2 5.0 %fusion.8 = bf16[128,2048]{1,0:T(8,128)(2,1)S(1)} fusion(bf16[1024,2048]{1,0:T(8,128)(2,1)} %get-tuple-element.41, bf16[128,2048]{1,0:T(8,128)(2,1)S(1)} %get-tuple-element.39, bf16[2048,1024]{1,0:T(8,128)(2,1)} %get-tuple-element.40), kind=kOutput, calls=%fused_computation.9 | convolution fusion | flops 1074921472 | bytes 9437184 | tf_op jit(solution)/shard_map/cond/branch_0_fun/dot_general | solution.py:63
  79.2 1.1 reshape.226
  80.3 6.5 %all-to-all-start.1 = ((bf16[64,2,2048]{2,1,0:T(2,128)(2,1)}), bf16[64,2,2048]{2,1,0:T(2,128)(2,1)S(1)}, u32[]{:S(2)}, u32[]{:S(2)}) async-start(bf16[64,2,2048]{2,1,0:T(2,128)(2,1)} %reshape.226), calls=%async_computation.1 | async-start | bytes 1048576 | tf_op jit(solution)/shard_map/all_to_all | solution.py:73
  87.9 20.1 %all-to-all-done.1 = bf16[64,2,2048]{2,1,0:T(2,128)(2,1)S(1)} async-done(((bf16[64,2,2048]{2,1,0:T(2,128)(2,1)}), bf16[64,2,2048]{2,1,0:T(2,128)(2,1)S(1)}, u32[]{:S(2)}, u32[]{:S(2)}) %all-to-all-start.1) | async-done | bytes 524320 | tf_op jit(solution)/shard_map/all_to_all | solution.py:73
  108.6 0.5 fusion.89
  109.5 1.1 broadcast_in_dim.11
  110.6 6.1 %all-to-all-start.2 = ((bf16[64,2,2048]{2,1,0:T(2,128)(2,1)}), bf16[64,2,2048]{2,1,0:T(2,128)(2,1)S(1)}, u32[]{:S(2)}, u32[]{:S(2)}) async-start(bf16[64,2,2048]{2,1,0:T(2,128)(2,1)} %bitcast.21), calls=%async_computation.2 | async-start | bytes 1048576 | tf_op jit(solution)/shard_map/all_to_all | solution.py:56
  116.7 21.5 %all-to-all-done.2 = bf16[64,2,2048]{2,1,0:T(2,128)(2,1)S(1)} async-done(((bf16[64,2,2048]{2,1,0:T(2,128)(2,1)}), bf16[64,2,2048]{2,1,0:T(2,128)(2,1)S(1)}, u32[]{:S(2)}, u32[]{:S(2)}) %all-to-all-start.2) | async-done | bytes 524320 | tf_op jit(solution)/shard_map/all_to_all | solution.py:56
  138.3 5.2 %conditional.5 = (bf16[128,2048]{1,0:T(8,128)(2,1)S(1)}) conditional(s32[]{:T(128)} %convert_element_type.187, (bf16[128,2048]{1,0:T(8,128)(2,1)S(1)}, bf16[2048,1024]{1,0:T(8,128)(2,1)}, bf16[1024,2048]{1,0:T(8,128)(2,1)}) %tuple.25, (bf16[128,2048]{1,0:T(8,128)(2,1)S(1)}, bf16[2048,1024]{1,0:T(8,128)(2,1)}, bf16[1024,2048]{1,0:T(8,128)(2,1)}) %tuple.41), branch_computations={%region_9.10_spmd, %region_10.11_spmd} | conditional | flops 1074921472 | bytes 9437192
  138.5 5.0 %fusion.62 = bf16[128,2048]{1,0:T(8,128)(2,1)S(1)} fusion(bf16[1024,2048]{1,0:T(8,128)(2,1)} %get-tuple-element.50, bf16[128,2048]{1,0:T(8,128)(2,1)S(1)} %get-tuple-element.48, bf16[2048,1024]{1,0:T(8,128)(2,1)} %get-tuple-element.49), kind=kOutput, calls=%fused_computation.63 | convolution fusion | flops 1074921472 | bytes 9437184 | tf_op jit(solution)/shard_map/cond/branch_1_fun/dot_general | solution.py:63
  143.5 1.1 reshape.229
  144.6 7.0 %all-to-all-start.3 = ((bf16[64,2,2048]{2,1,0:T(2,128)(2,1)}), bf16[64,2,2048]{2,1,0:T(2,128)(2,1)S(1)}, u32[]{:S(2)}, u32[]{:S(2)}) async-start(bf16[64,2,2048]{2,1,0:T(2,128)(2,1)} %reshape.229), calls=%async_computation.3 | async-start | bytes 1048576 | tf_op jit(solution)/shard_map/all_to_all | solution.py:73
  152.1 24.2 %all-to-all-done.3 = bf16[64,2,2048]{2,1,0:T(2,128)(2,1)S(1)} async-done(((bf16[64,2,2048]{2,1,0:T(2,128)(2,1)}), bf16[64,2,2048]{2,1,0:T(2,128)(2,1)S(1)}, u32[]{:S(2)}, u32[]{:S(2)}) %all-to-all-start.3) | async-done | bytes 524320 | tf_op jit(solution)/shard_map/all_to_all | solution.py:73
  177.3 1.9 %collective-permute-start.3 = (bf16[64,2048]{1,0:T(8,128)(2,1)S(1)}, bf16[64,2048]{1,0:T(8,128)(2,1)S(1)}, u32[]{:S(2)}, u32[]{:S(2)}) collective-permute-start(bf16[64,2048]{1,0:T(8,128)(2,1)S(1)} %get-tuple-element.61), channel_id=1, source_target_pairs={{0,512},{512,0},{1,513},{513,1},{2,514},{514,2},{3,515},{515,3},{4... | collective-permute-start | bytes 786440 | tf_op jit(solution)/shard_map/ppermute | solution.py:92
  179.2 1.5 collective-permute-done.3
  180.7 0.9 maximum_select_fusion
  (43 shorter events, 4.4 us)
Async XLA Ops:
  2.3 21.5 %collective-permute-start = (f32[10,2048]{1,0:T(8,128)S(1)}, f32[10,2048]{1,0:T(8,128)S(1)}, u32[]{:S(2)}, u32[]{:S(2)}) collective-permute-start(f32[10,2048]{1,0:T(8,128)S(1)} %select_maximum_fusion), channel_id=1, source_target_pairs={{0,512},{512,0},{1,513},{513,1},{2,514},{514,2},{3,515},{515,3},{4... | collective-permute-start | bytes 245768 | tf_op jit(solution)/shard_map/ppermute | solution.py:92
  18.3 55.8 %collective-permute-start.1 = (bf16[2048,1024]{1,0:T(8,128)(2,1)}, bf16[2048,1024]{1,0:T(8,128)(2,1)}, u32[]{:S(2)}, u32[]{:S(2)}) collective-permute-start(bf16[2048,1024]{1,0:T(8,128)(2,1)} %bitcast.86), channel_id=1, source_target_pairs={{0,512},{512,0},{1,513},{513,1},{2,514},{514,2},{3,515},{515,3},{4... | collective-permute-start | bytes 12582920 | tf_op jit(solution)/shard_map/ppermute | solution.py:92
  20.2 53.9 %collective-permute-start.2 = (bf16[1024,2048]{1,0:T(8,128)(2,1)}, bf16[1024,2048]{1,0:T(8,128)(2,1)}, u32[]{:S(2)}, u32[]{:S(2)}) collective-permute-start(bf16[1024,2048]{1,0:T(8,128)(2,1)} %bitcast.89), channel_id=1, source_target_pairs={{0,512},{512,0},{1,513},{513,1},{2,514},{514,2},{3,515},{515,3},{4... | collective-permute-start | bytes 12582920 | tf_op jit(solution)/shard_map/ppermute | solution.py:92
  44.0 29.9 %all-to-all-start = ((bf16[64,2,2048]{2,1,0:T(2,128)(2,1)}), bf16[64,2,2048]{2,1,0:T(2,128)(2,1)S(1)}, u32[]{:S(2)}, u32[]{:S(2)}) async-start(bf16[64,2,2048]{2,1,0:T(2,128)(2,1)} %bitcast.8), calls=%async_computation | async-start | bytes 1048576 | tf_op jit(solution)/shard_map/all_to_all | solution.py:56
  74.2 13.3 %copy-start = (bf16[2,64,2048]{2,1,0:T(8,128)(2,1)S(1)}, bf16[2,64,2048]{2,1,0:T(8,128)(2,1)}, u32[]{:S(2)}) copy-start(bf16[2,64,2048]{2,1,0:T(8,128)(2,1)} %param.10) | copy-start | bytes 1572868
  80.3 27.7 %all-to-all-start.1 = ((bf16[64,2,2048]{2,1,0:T(2,128)(2,1)}), bf16[64,2,2048]{2,1,0:T(2,128)(2,1)S(1)}, u32[]{:S(2)}, u32[]{:S(2)}) async-start(bf16[64,2,2048]{2,1,0:T(2,128)(2,1)} %reshape.226), calls=%async_computation.1 | async-start | bytes 1048576 | tf_op jit(solution)/shard_map/all_to_all | solution.py:73
  110.6 27.5 %all-to-all-start.2 = ((bf16[64,2,2048]{2,1,0:T(2,128)(2,1)}), bf16[64,2,2048]{2,1,0:T(2,128)(2,1)S(1)}, u32[]{:S(2)}, u32[]{:S(2)}) async-start(bf16[64,2,2048]{2,1,0:T(2,128)(2,1)} %bitcast.21), calls=%async_computation.2 | async-start | bytes 1048576 | tf_op jit(solution)/shard_map/all_to_all | solution.py:56
  144.6 31.6 %all-to-all-start.3 = ((bf16[64,2,2048]{2,1,0:T(2,128)(2,1)}), bf16[64,2,2048]{2,1,0:T(2,128)(2,1)S(1)}, u32[]{:S(2)}, u32[]{:S(2)}) async-start(bf16[64,2,2048]{2,1,0:T(2,128)(2,1)} %reshape.229), calls=%async_computation.3 | async-start | bytes 1048576 | tf_op jit(solution)/shard_map/all_to_all | solution.py:73
  177.3 3.4 %collective-permute-start.3 = (bf16[64,2048]{1,0:T(8,128)(2,1)S(1)}, bf16[64,2048]{1,0:T(8,128)(2,1)S(1)}, u32[]{:S(2)}, u32[]{:S(2)}) collective-permute-start(bf16[64,2048]{1,0:T(8,128)(2,1)S(1)} %get-tuple-element.61), channel_id=1, source_target_pairs={{0,512},{512,0},{1,513},{513,1},{2,514},{514,2},{3,515},{515,3},{4... | collective-permute-start | bytes 786440 | tf_op jit(solution)/shard_map/ppermute | solution.py:92
